TPU v7x, 32 devices: a whole 2x2x4 slice. The times are simulated.
32 devices in a mesh: section: 2 (over x), tensor: 8 (over z, core), dp: 2 (over y).
Axes of the slice: x: 2, y: 2, z: 4, core: 2. Of those that a mesh axis runs over, the one named last changes fastest.
Arguments:
- dec_queries: bfloat16 [2, 4, 512, 8192], P('section', 'dp', None, 'tensor'), may hold values from -8 to 8
- enc_keys: bfloat16 [2, 4, 512, 8192], P('section', 'dp', None, 'tensor'), may hold values from -4 to 4
- enc_values: bfloat16 [2, 4, 512, 8192], P('section', 'dp', None, 'tensor'), may hold values from -4 to 4
- out_grad: bfloat16 [2, 4, 512, 8192], P('section', 'dp', None, 'tensor'), may hold values from -15 to 15
- key_weight: bfloat16 [2, 1024, 8192], P('section', None, 'tensor'), may hold values from -0.1875 to 0.1875
- value_weight: bfloat16 [2, 1024, 8192], P('section', None, 'tensor'), may hold values from -0.1875 to 0.1875
- enc_hidden: float32 [4, 512, 1024], P('dp', 'section', 'tensor'), may hold values from -2 to 2, as said below
- enc_gain: float32 [1024], P('tensor'), may hold values from 0.1 to 1.9
Outputs:
- enc_input_grad: float32 [4, 512, 1024], P('dp', 'section', 'tensor')
Inputs may be any that keep to these rules, and one draw needn't show every extreme that they name: `enc_hidden`: every entry's magnitude is at least 0.25.
All inputs are finite; a program needn't handle non-finite values.
Results may differ from a plain program's by a relative error of at most 0.0041.
Values sent between devices are 32-bit elements; how exact they have to be, the bound alone decides.
A program may use at most 128 MiB of HBM per device.

v0:
```python
import jax
import jax.numpy as jnp
from jax import lax
from jax.sharding import PartitionSpec as P

D = 1024
DK = 128


epsilon = 1e-06


def per_device(
    dec_queries, enc_keys, enc_values, out_grad, key_weight, value_weight, enc_hidden, enc_gain
):
    seqs_here = dec_queries.shape[1]
    dec_len = dec_queries.shape[2]
    hidden_here = dec_queries.shape[3]
    enc_len = enc_keys.shape[2]
    heads_here = hidden_here // DK
    model_width = key_weight.shape[1]
    square_total = lax.psum(jnp.sum(enc_hidden * enc_hidden, axis=-1), "tensor")
    query_heads = dec_queries[0].reshape(seqs_here, dec_len, heads_here, DK)
    key_heads = enc_keys[0].reshape(seqs_here, enc_len, heads_here, DK)
    value_heads = enc_values[0].reshape(seqs_here, enc_len, heads_here, DK)
    grad_heads = out_grad[0].reshape(seqs_here, dec_len, heads_here, DK)
    scores = jnp.einsum(
        "bqhd,bkhd->bhqk", query_heads, key_heads, preferred_element_type=jnp.float32
    )
    shifted = jnp.exp(scores - jnp.max(scores, axis=-1, keepdims=True))
    attn_probs = shifted / jnp.sum(shifted, axis=-1, keepdims=True)
    probs_low = attn_probs.astype(jnp.bfloat16)
    attended = jnp.einsum(
        "bhqk,bkhd->bqhd", probs_low, value_heads, preferred_element_type=jnp.float32
    )
    row_dot = jnp.sum(grad_heads.astype(jnp.float32) * attended, axis=-1)
    value_grad = jnp.einsum(
        "bhqk,bqhd->bkhd", probs_low, grad_heads, preferred_element_type=jnp.float32
    ).astype(jnp.bfloat16)
    prob_grad = jnp.einsum(
        "bqhd,bkhd->bhqk", grad_heads, value_heads, preferred_element_type=jnp.float32
    )
    score_low = (attn_probs * (prob_grad - jnp.transpose(row_dot, (0, 2, 1))[..., None])).astype(
        jnp.bfloat16
    )
    key_grad = jnp.einsum(
        "bhqk,bqhd->bkhd", score_low, query_heads, preferred_element_type=jnp.float32
    ).astype(jnp.bfloat16)
    flat_rows = seqs_here * enc_len
    partial_value = jnp.einsum(
        "th,dh->td",
        key_grad.reshape(flat_rows, hidden_here),
        key_weight[0],
        preferred_element_type=jnp.float32,
    )
    partial_value = partial_value + jnp.einsum(
        "th,dh->td",
        value_grad.reshape(flat_rows, hidden_here),
        value_weight[0],
        preferred_element_type=jnp.float32,
    )
    partial_value = partial_value.reshape(seqs_here, enc_len, model_width)
    head_part = lax.psum_scatter(partial_value, "tensor", scatter_dimension=2, tiled=True)
    enc_grad = lax.psum_scatter(head_part, "section", scatter_dimension=1, tiled=True)
    scaled = enc_gain * enc_grad
    cross_local = jnp.sum(scaled * enc_hidden, axis=-1)
    cross_total = lax.psum(cross_local, "tensor")
    inverse = lax.rsqrt(square_total / D + epsilon)
    return (
        scaled * inverse[..., None]
        - enc_hidden * (cross_total * inverse * inverse * inverse / D)[..., None]
    )


def solution(mesh):
    return jax.shard_map(
        per_device,
        mesh=mesh,
        in_specs=(
            P("section", "dp", None, "tensor"),
            P("section", "dp", None, "tensor"),
            P("section", "dp", None, "tensor"),
            P("section", "dp", None, "tensor"),
            P("section", None, "tensor"),
            P("section", None, "tensor"),
            P("dp", "section", "tensor"),
            P("tensor"),
        ),
        out_specs=P("dp", "section", "tensor"),
        check_vma=False,
    )
```

profile of v0, /device:TPU:0, one launch (start us, length us, event | category | flops | bytes accessed | tf_op | source)
XLA Modules:
  0.0 159.6 jit_solution(9555363609104835648)
XLA Ops:
  6.5 0.0 copy-start
  6.5 0.0 reduce-scatter.3.cloned.1.call-start
  6.5 3.7 %copy.40 = bf16[128,8,8,128]{3,2,1,0:T(8,128)(2,1)} copy(bf16[128,8,8,128]{3,1,2,0:T(8,128)(2,1)} %bitcast.55) | data formatting | bytes 4194304
  10.3 0.0 copy-done.3
  10.3 2.0 %copy.41 = bf16[128,8,8,128]{3,2,1,0:T(8,128)(2,1)} copy(bf16[128,8,8,128]{3,1,2,0:T(8,128)(2,1)S(1)} %bitcast.56) | data formatting | bytes 4194304
  12.2 3.9 %copy.39 = bf16[1,2,512,1024]{2,3,1,0:T(8,128)(2,1)} copy(bf16[1,2,512,1024]{3,2,1,0:T(8,128)(2,1)} %param.10) | data formatting | bytes 4194304 | tf_op jit(solution)/shard_map/reshape;squeeze | solution.py:25
  16.2 3.9 %copy.21 = bf16[1,2,512,1024]{2,3,1,0:T(8,128)(2,1)} copy(bf16[1,2,512,1024]{3,2,1,0:T(8,128)(2,1)} %param.11) | data formatting | bytes 4194304 | tf_op args[3]
  20.1 10.7 %fusion.29 = (f32[2,8,512]{2,1,0:T(8,128)S(1)}, f32[2,8,512,512]{2,3,1,0:T(8,128)}) fusion(bf16[2,512,8,128]{3,2,1,0:T(8,128)(2,1)} %bitcast.60, bf16[2,512,8,128]{3,2,1,0:T(8,128)(2,1)} %bitcast.57), kind=kOutput, calls=%fused_computation.31 | convolution fusion | flops 1082130944 | bytes 21004288 | tf_op jit(solution)/shard_map/sub | solution.py:30
  30.8 6.8 %fusion.3 = bf16[2,8,512,512]{2,3,1,0:T(8,128)(2,1)S(1)} fusion(f32[2,8,512,512]{2,3,1,0:T(8,128)} %get-tuple-element.12, f32[2,8,512]{2,1,0:T(8,128)S(1)} %get-tuple-element.11), kind=kLoop, calls=%fused_computation.6 | loop fusion | flops 8388608 | bytes 25198592 | tf_op jit(solution)/shard_map/convert_element_type | solution.py:32
  37.6 0.0 copy-done.2
  37.6 0.0 copy-start.1
  37.6 2.3 %convert_bitcast_fusion = bf16[2,512,8,128]{3,1,2,0:T(8,128)(2,1)S(1)} fusion(bf16[2,8,512,512]{2,3,1,0:T(8,128)(2,1)S(1)} %fusion.3, bf16[2,512,8,128]{1,3,2,0:T(8,128)(2,1)S(1)} %bitcast.52), kind=kOutput, calls=%fused_computation.20 | convolution fusion | flops 1074790400 | bytes 12582912 | tf_op jit(solution)/shard_map/bhqk,bqhd->bkhd/dot_general | solution.py:37
  40.0 0.0 copy-done.1
  40.0 1.3 fusion.6
  41.3 2.7 %copy.32 = bf16[2,512,8,128]{3,2,1,0:T(8,128)(2,1)} copy(bf16[2,512,8,128]{3,1,2,0:T(8,128)(2,1)S(1)} %convert_bitcast_fusion) | data formatting | bytes 4194304 | tf_op jit(solution)/shard_map/convert_element_type | solution.py:39
  44.0 11.6 %convert_bitcast_fusion.1 = bf16[2,512,8,128]{3,1,2,0:T(8,128)(2,1)} fusion(f32[2,8,512]{2,1,0:T(8,128)S(1)} %bitcast.62, f32[2,8,512,512]{2,3,1,0:T(8,128)} %get-tuple-element.12, f32[2,8,512]{2,1,0:T(8,128)S(1)} %get-tuple-element.11, bf16[2,512,8,128]{1,3,2,0:T(8,128)(2,1)} %bitcast.49, bf16[2,512,8,128]{1,3,2,0:T(8,128)(2,1)} %bitcast.51, ...), kind=kOutput, calls=%fused_computation.21 | convolution fusion | flops 2165309440 | bytes 25231360 | tf_op jit(solution)/shard_map/bhqk,bqhd->bkhd/dot_general | solution.py:46
  55.5 3.1 %copy.30 = bf16[2,512,8,128]{3,2,1,0:T(8,128)(2,1)S(1)} copy(bf16[2,512,8,128]{3,1,2,0:T(8,128)(2,1)} %convert_bitcast_fusion.1) | data formatting | bytes 4194304 | tf_op jit(solution)/shard_map/convert_element_type | solution.py:48
  58.6 0.0 copy-done
  58.7 0.0 copy-done.4
  58.7 0.0 copy-start.7
  58.7 2.4 %fusion.7 = f32[1024,1024]{1,0:T(8,128)S(1)} fusion(bf16[128,8,8,128]{3,2,1,0:T(8,128)(2,1)S(1)} %bitcast.59, bf16[1,1024,1024]{2,1,0:T(8,128)(2,1)S(1)} %copy-done), kind=kOutput, calls=%fused_computation.10 | convolution fusion | flops 2147483648 | bytes 8388608 | tf_op jit(solution)/shard_map/th,dh->td/dot_general | solution.py:56
  61.0 0.0 copy-done.7
  61.1 4.3 %fusion.17 = f32[1024,1024]{1,0:T(8,128)} fusion(f32[1024,1024]{1,0:T(8,128)S(1)} %fusion.7, bf16[1,1024,1024]{2,1,0:T(8,128)(2,1)S(1)} %copy-done.7, bf16[128,8,8,128]{3,2,1,0:T(8,128)(2,1)S(1)} %bitcast.61), kind=kOutput, calls=%fused_computation.22 | convolution fusion | flops 2148532224 | bytes 12582912 | tf_op jit(solution)/shard_map/th,dh->td/dot_general | solution.py:50
  65.3 0.0 reduce-scatter.3.cloned.1.call-update
  65.4 0.0 reduce-scatter.5.cloned.1.call-start
  65.4 52.8 %reduce-scatter.3.cloned.1.call-done = f32[2,512,128]{2,1,0:T(8,128)} async-done(((f32[2,512,1024]{2,1,0:T(8,128)}), f32[2,512,128]{2,1,0:T(8,128)}) %reduce-scatter.3.cloned.1.call-update) | async-done | bytes 524304 | tf_op jit(solution)/shard_map/reduce_scatter | solution.py:63
  118.2 0.0 reduce-scatter.5.cloned.1.call-update
  118.2 15.4 %reduce-scatter.5.cloned.1.call-done = f32[2,256,128]{2,1,0:T(8,128)} async-done(((f32[2,512,128]{2,1,0:T(8,128)}), f32[2,256,128]{2,1,0:T(8,128)}) %reduce-scatter.5.cloned.1.call-update) | async-done | bytes 262160 | tf_op jit(solution)/shard_map/reduce_scatter | solution.py:64
  133.6 0.0 copy-done.5
  133.6 1.2 multiply_reduce_fusion.1
  134.7 16.2 %all-reduce = (f32[2,256]{1,0:T(2,128)S(1)}, f32[2,256]{1,0:T(2,128)S(1)}) all-reduce(f32[2,256]{1,0:T(2,128)S(1)} %get-tuple-element.6, f32[2,256]{1,0:T(2,128)S(1)} %get-tuple-element.5), channel_id=1, replica_groups=mesh['section'=2,'tensor'=8,'dp'=2] {'tensor'}, use_global_device_ids=true, to_apply=%region_8.0 | all-reduce | flops 1024 | bytes 8192 | tf_op jit(solution)/shard_map/psum | solution.py:67
  150.9 1.9 %multiply_subtract_fusion = f32[2,256,128]{2,1,0:T(8,128)} fusion(f32[2,256,128]{2,1,0:T(8,128)S(1)} %copy-done.5, f32[2,256,128]{2,1,0:T(8,128)} %reduce-scatter.5.cloned.1.call-done, f32[2,256]{1,0:T(2,128)S(1)} %get-tuple-element.10, f32[2,256]{1,0:T(2,128)S(1)} %get-tuple-element.9, f32[128]{0:T(128)S(1)} %copy-done.6), kind=kLoop, calls=%fused_computation.25 | loop fusion | flops 262144 | bytes 791040 | tf_op jit(solution)/shard_map/sub | solution.py:70
  (7 shorter events, 0.0 us)
Async XLA Ops:
  6.5 52.1 %copy-start = (bf16[1,1024,1024]{2,1,0:T(8,128)(2,1)S(1)}, bf16[1,1024,1024]{2,1,0:T(8,128)(2,1)}, u32[]{:S(2)}) copy-start(bf16[1,1024,1024]{2,1,0:T(8,128)(2,1)} %param.13) | copy-start | bytes 6291460
  6.5 111.6 %reduce-scatter.3.cloned.1.call-start = ((), (), s32[]{:S(2)}) async-start(), calls=%async_computation.2 | async-start | bytes 4718592 | tf_op jit(solution)/shard_map/reduce_scatter | solution.py:63
  6.5 3.7 %copy-start.3 = (bf16[1,2,512,1024]{3,2,1,0:T(8,128)(2,1)S(1)}, bf16[1,2,512,1024]{3,2,1,0:T(8,128)(2,1)}, u32[]{:S(2)}) copy-start(bf16[1,2,512,1024]{3,2,1,0:T(8,128)(2,1)} %param.9) | copy-start | bytes 6291460
  30.8 6.9 %copy-start.2 = (bf16[1,2,512,1024]{2,3,1,0:T(8,128)(2,1)S(1)}, bf16[1,2,512,1024]{2,3,1,0:T(8,128)(2,1)}, u32[]{:S(2)}) copy-start(bf16[1,2,512,1024]{2,3,1,0:T(8,128)(2,1)} %copy.21) | copy-start | bytes 6291460
  37.6 2.4 %copy-start.1 = (bf16[1,2,512,1024]{2,3,1,0:T(8,128)(2,1)S(1)}, bf16[1,2,512,1024]{2,3,1,0:T(8,128)(2,1)}, u32[]{:S(2)}) copy-start(bf16[1,2,512,1024]{2,3,1,0:T(8,128)(2,1)} %copy.39) | copy-start | bytes 6291460
  55.5 3.1 %copy-start.4 = (bf16[2,512,8,128]{3,2,1,0:T(8,128)(2,1)S(1)}, bf16[2,512,8,128]{3,2,1,0:T(8,128)(2,1)}, u32[]{:S(2)}) copy-start(bf16[2,512,8,128]{3,2,1,0:T(8,128)(2,1)} %copy.32) | copy-start | bytes 6291460
  58.7 2.4 %copy-start.7 = (bf16[1,1024,1024]{2,1,0:T(8,128)(2,1)S(1)}, bf16[1,1024,1024]{2,1,0:T(8,128)(2,1)}, u32[]{:S(2)}) copy-start(bf16[1,1024,1024]{2,1,0:T(8,128)(2,1)} %param.12) | copy-start | bytes 6291460
  65.3 68.2 %copy-start.5 = (f32[2,256,128]{2,1,0:T(8,128)S(1)}, f32[2,256,128]{2,1,0:T(8,128)}, u32[]{:S(2)}) copy-start(f32[2,256,128]{2,1,0:T(8,128)} %param.14) | copy-start | bytes 786436
  65.3 68.2 %copy-start.6 = (f32[128]{0:T(128)S(1)}, f32[128]{0:T(128)}, u32[]{:S(2)}) copy-start(f32[128]{0:T(128)} %param.15) | copy-start | bytes 1540
  65.4 68.2 %reduce-scatter.5.cloned.1.call-start = ((), (), s32[]{:S(2)}) async-start(), calls=%async_computation.3 | async-start | bytes 786432 | tf_op jit(solution)/shard_map/reduce_scatter | solution.py:64
Sparse Core Ops, SparseCore 0:
  65.5 52.6 reduce-scatter.2
  120.4 13.0 reduce-scatter.4
where the time goes:
time: 160 us
  waiting for transfers between devices  68.1 us (43%)
  matrix products  32.5 us (20%)
  local copies, waits for them, and re-layouts  19.4 us (12%)
  blocking collectives  16.2 us (10%)
  between operations  13.5 us (8%)
  other arithmetic  9.88 us (6%)
    reduce_scatter x1, waiting for transfers between devices, per_device(): lax.psum_scatter(partial_value, 'tensor', scatter_dimension=2, tiled=True)  52.8 us
    psum x1, blocking collectives, per_device(): cross_total = lax.psum(cross_local, 'tensor')  16.2 us
    reduce_scatter x1, waiting for transfers between devices, per_device(): lax.psum_scatter(head_part, 'section', scatter_dimension=1, tiled=True)  15.4 us
    dot_general x1, matrix products, per_device(): jnp.einsum('bhqk,bqhd->bkhd', score_low, query_heads, preferred_element_t...  11.6 us
    sub x1, matrix products, per_device(): shifted = jnp.exp(scores - jnp.max(scores, axis=-1, keepdims=True))  10.7 us
    unnamed x19, local copies, waits for them, and re-layouts  9.66 us
    convert_element_type x1, other arithmetic, per_device(): probs_low = attn_probs.astype(jnp.bfloat16)  6.84 us
    dot_general x1, matrix products, per_device(): jnp.einsum('th,dh->td', key_grad.reshape(flat_rows, hidden_here), key_wei...  4.29 us
  transfers between devices with their start and end apart: 2, of which 2 were waited for; matrix products, arithmetic and copies ran while one was open for 0% of the time, Pallas kernels for 0%

commit v1 on v0

v1 whole, which is shorter than its diff:
```python
import functools

import jax
import jax.numpy as jnp
from jax import lax
from jax.experimental import pallas as pl
from jax.experimental.pallas import tpu as pltpu
from jax.sharding import PartitionSpec as P

DK = 128
CORES = 2
EPSILON = 1e-06
MESH = pl.DeviceIdType.MESH
F32 = jnp.float32
BF16 = jnp.bfloat16
QUERY_BLOCK = 256


def dot_nt(a, b, precision=None):
    return lax.dot_general(
        a, b, (((1,), (1,)), ((), ())), precision=precision, preferred_element_type=F32
    )


def dot_nn(a, b):
    return lax.dot_general(a, b, (((1,), (0,)), ((), ())), preferred_element_type=F32)


def dot_tn(a, b, precision=None):
    return lax.dot_general(
        a, b, (((0,), (0,)), ((), ())), precision=precision, preferred_element_type=F32
    )


def body(
    sections, tensors, query_block,
    q_hbm, k_hbm, v_hbm, g_hbm, wk_hbm, wv_hbm, hidden_hbm, gain_hbm,
    out_ref,
    q_buf, k_buf, v_buf, g_buf, w_buf, hidden, gain, grads,
    part, pair_in, section_in, line_out, line_in,
    square_out, square_in, cross_out, cross_in,
    load_sem, weight_sem, small_sem,
    pair_send, pair_recv, section_send, section_recv, line_send, line_recv,
    square_send, square_recv, cross_send, cross_recv,
):
    seqs, heads, dec_len, _ = q_buf.shape
    enc_len = k_buf.shape[2]
    inner = heads * DK
    model_width = w_buf.shape[0]
    feats = out_ref.shape[2]
    rows = out_ref.shape[1]
    chips = tensors // CORES
    s_me = lax.axis_index("section")
    t_me = lax.axis_index("tensor")
    z_me = lax.div(t_me, CORES)
    c_me = lax.rem(t_me, CORES)
    partner = z_me * CORES + (CORES - 1 - c_me)

    def loads(b, h):
        cols = pl.ds(pl.multiple_of(h * DK, DK), DK)
        return [
            pltpu.make_async_copy(src.at[0, b, :, cols], dst.at[b, h], load_sem.at[i, b, h])
            for i, (src, dst) in enumerate(
                ((q_hbm, q_buf), (k_hbm, k_buf), (v_hbm, v_buf), (g_hbm, g_buf))
            )
        ]

    def start_loads(b):
        def step(h, carry):
            for copy in loads(b, h):
                copy.start()
            return carry

        lax.fori_loop(0, heads, step, 0)

    weight_copies = [
        pltpu.make_async_copy(src.at[0], w_buf.at[:, pl.ds(i * inner, inner)], weight_sem.at[i])
        for i, src in enumerate((wk_hbm, wv_hbm))
    ]
    small_copies = [
        pltpu.make_async_copy(hidden_hbm, hidden, small_sem.at[0]),
        pltpu.make_async_copy(gain_hbm, gain, small_sem.at[1]),
    ]

    start_loads(0)
    for copy in small_copies + weight_copies:
        copy.start()
    for b in range(1, seqs):
        start_loads(b)

    barrier = pltpu.get_barrier_semaphore()
    for i in range(1, tensors):
        pl.semaphore_signal(
            barrier, inc=1, device_id={"tensor": lax.rem(t_me + i, tensors)}, device_id_type=MESH
        )
    for i in range(1, sections):
        pl.semaphore_signal(
            barrier, inc=1, device_id={"section": lax.rem(s_me + i, sections)}, device_id_type=MESH
        )

    def head(b, h):
        for copy in loads(b, h):
            copy.wait()
        keys = k_buf[b, h]
        values = v_buf[b, h]
        key_grad = None
        for start in range(0, dec_len, query_block):
            queries = q_buf[b, h, pl.ds(start, query_block), :]
            out_grads = g_buf[b, h, pl.ds(start, query_block), :]
            scores = dot_nt(keys, queries)
            shifted = jnp.exp(scores - jnp.max(scores, axis=0, keepdims=True))
            probs = shifted * (1.0 / jnp.sum(shifted, axis=0, keepdims=True))
            probs_low = probs.astype(BF16)
            prob_grad = dot_nt(values, out_grads)
            row_dot = jnp.sum(probs_low.astype(F32) * prob_grad, axis=0, keepdims=True)
            score_low = (probs * (prob_grad - row_dot)).astype(BF16)
            value_term = dot_nn(probs_low, out_grads)
            key_term = dot_nn(score_low, queries)
            if key_grad is None:
                key_grad, value_grad = key_term, value_term
            else:
                key_grad, value_grad = key_grad + key_term, value_grad + value_term
        grads[:, pl.ds(pl.multiple_of(h * DK, DK), DK)] = key_grad.astype(BF16)
        grads[:, pl.ds(pl.multiple_of(inner + h * DK, DK), DK)] = value_grad.astype(BF16)

    def pair_copy(b, k):
        return pltpu.make_async_remote_copy(
            src_ref=part.at[b, k, CORES - 1 - c_me], dst_ref=pair_in.at[b, k],
            send_sem=pair_send.at[b, k], recv_sem=pair_recv.at[b, k],
            device_id={"tensor": partner}, device_id_type=MESH,
        )

    def section_copies(b, k):
        copies = []
        for i in range(1, sections):
            target = lax.rem(s_me + i, sections)
            copies.append(pltpu.make_async_remote_copy(
                src_ref=part.at[b, k, c_me, target], dst_ref=section_in.at[b, k, i - 1],
                send_sem=section_send.at[b, k, i - 1], recv_sem=section_recv.at[b, k, i - 1],
                device_id={"section": target}, device_id_type=MESH,
            ))
        return copies

    def line_copy(b, k):
        target = lax.rem(z_me + 1 + k, chips) * CORES + c_me
        return pltpu.make_async_remote_copy(
            src_ref=line_out.at[b, k], dst_ref=line_in.at[b, k],
            send_sem=line_send.at[b, k], recv_sem=line_recv.at[b, k],
            device_id={"tensor": target}, device_id_type=MESH,
        )

    def stat_copies(src, dst, send, recv):
        return [
            pltpu.make_async_remote_copy(
                src_ref=src, dst_ref=dst.at[i - 1],
                send_sem=send.at[i - 1], recv_sem=recv.at[i - 1],
                device_id={"tensor": lax.rem(t_me + i, tensors)}, device_id_type=MESH,
            )
            for i in range(1, tensors)
        ]

    def square_copies():
        return stat_copies(square_out, square_in, square_send, square_recv)

    def cross_copies(b):
        return stat_copies(
            cross_out.at[b], cross_in.at[b], cross_send.at[b], cross_recv.at[b]
        )

    def lane_sums(x):
        total = dot_nt(jnp.ones((8, feats), F32), x, lax.Precision.HIGHEST)
        return total[0:1, :]

    def spread(row):
        return dot_tn(
            jnp.broadcast_to(row, (8, rows)), jnp.full((8, feats), 0.125, F32),
            lax.Precision.HIGHEST,
        )

    def project(b, k):
        chip = lax.rem(z_me + 1 + k, chips)
        width = CORES * feats
        block = dot_nt(
            grads[...], w_buf[pl.ds(pl.multiple_of(chip * width, width), width), :]
        )
        for half in range(CORES):
            part[b, k, half] = block[:, half * feats : (half + 1) * feats].reshape(
                sections, rows, feats
            )
        pair_copy(b, k).start()

    def pair_step(b, k):
        pair_copy(b, k).wait_recv()
        part[b, k, c_me] = part[b, k, c_me] + pair_in[b, k]
        for copy in section_copies(b, k):
            copy.start()

    def section_step(b, k):
        total = part[b, k, c_me, s_me]
        for i, copy in enumerate(section_copies(b, k)):
            copy.wait_recv()
            total = total + section_in[b, k, i]
        line_out[b, k] = total

    def loop(low, high, step):
        def run(i, carry):
            step(i)
            return carry

        lax.fori_loop(low, high, run, 0)

    def forward(b, k):
        section_step(b, k)
        line_copy(b, k).start()

    def finish_sum(b):
        section_step(b, chips - 1)
        total = line_out[b, chips - 1]
        for k in range(chips - 1):
            line_copy(b, k).wait_recv()
            total = total + line_in[b, k]
        scaled = gain[...] * total
        out_ref[b] = scaled
        cross_out[b] = lane_sums(scaled * hidden[b])
        for copy in cross_copies(b):
            copy.start()

    def finish_norm(b):
        for copy in cross_copies(b):
            copy.wait_recv()
        cross = cross_out[b]
        square = square_out[b]
        for i in range(tensors - 1):
            cross = cross + cross_in[b, i]
            square = square + square_in[i, b]
        inverse = lax.rsqrt(square / model_width + EPSILON)
        factor = cross * inverse * inverse * inverse / model_width
        out_ref[b] = out_ref[b] * spread(inverse) - hidden[b] * spread(factor)

    heads_per_step = heads // chips
    for b in range(seqs):
        def heads_step(k):
            loop(0, heads_per_step, lambda i: head(b, k * heads_per_step + i))
            if b > 0:
                @pl.when(k < chips - 1)
                def _():
                    forward(b - 1, k)

        if b == 0:
            loop(0, heads, lambda h: head(b, h))
            for copy in small_copies:
                copy.wait()
            for i in range(seqs):
                square_out[i] = lane_sums(hidden[i] * hidden[i])
            for copy in weight_copies:
                copy.wait()
            pl.semaphore_wait(barrier, tensors - 1 + sections - 1)
            for copy in square_copies():
                copy.start()
        else:
            loop(0, chips, heads_step)

        project(b, 0)

        def project_step(k):
            project(b, k)
            pair_step(b, k - 1)

        loop(1, chips, project_step)
        pair_step(b, chips - 1)

    for copy in square_copies():
        copy.wait_recv()
    for b in range(seqs - 1):
        finish_sum(b)
    loop(0, chips - 1, lambda k: forward(seqs - 1, k))
    finish_sum(seqs - 1)
    for b in range(seqs):
        finish_norm(b)

    for copy in square_copies():
        copy.wait_send()
    for b in range(seqs):
        for copy in cross_copies(b):
            copy.wait_send()

        def drain(k):
            pair_copy(b, k).wait_send()
            for copy in section_copies(b, k):
                copy.wait_send()

        loop(0, chips, drain)
        loop(0, chips - 1, lambda k: line_copy(b, k).wait_send())


def per_device(
    sections, tensors,
    dec_queries, enc_keys, enc_values, out_grad, key_weight, value_weight, enc_hidden, enc_gain,
):
    _, seqs, dec_len, inner = dec_queries.shape
    enc_len = enc_keys.shape[2]
    heads = inner // DK
    model_width = key_weight.shape[1]
    chips = tensors // CORES
    feats = model_width // tensors
    rows = enc_len // sections
    dma = pltpu.SemaphoreType.DMA
    call = pl.pallas_call(
        functools.partial(body, sections, tensors, min(QUERY_BLOCK, dec_len)),
        out_shape=jax.ShapeDtypeStruct((seqs, rows, feats), F32),
        in_specs=[pl.BlockSpec(memory_space=pl.ANY)] * 8,
        out_specs=pl.BlockSpec(memory_space=pltpu.VMEM),
        scratch_shapes=[
            pltpu.VMEM((seqs, heads, dec_len, DK), BF16),
            pltpu.VMEM((seqs, heads, enc_len, DK), BF16),
            pltpu.VMEM((seqs, heads, enc_len, DK), BF16),
            pltpu.VMEM((seqs, heads, dec_len, DK), BF16),
            pltpu.VMEM((model_width, 2 * inner), BF16),
            pltpu.VMEM((seqs, rows, feats), F32),
            pltpu.VMEM((1, feats), F32),
            pltpu.VMEM((enc_len, 2 * inner), BF16),
            pltpu.VMEM((seqs, chips, CORES, sections, rows, feats), F32),
            pltpu.VMEM((seqs, chips, sections, rows, feats), F32),
            pltpu.VMEM((seqs, chips, sections - 1, rows, feats), F32),
            pltpu.VMEM((seqs, chips, rows, feats), F32),
            pltpu.VMEM((seqs, chips - 1, rows, feats), F32),
            pltpu.VMEM((seqs, 1, rows), F32),
            pltpu.VMEM((tensors - 1, seqs, 1, rows), F32),
            pltpu.VMEM((seqs, 1, rows), F32),
            pltpu.VMEM((seqs, tensors - 1, 1, rows), F32),
            dma((4, seqs, heads)),
            dma((2,)),
            dma((2,)),
            dma((seqs, chips)),
            dma((seqs, chips)),
            dma((seqs, chips, sections - 1)),
            dma((seqs, chips, sections - 1)),
            dma((seqs, chips - 1)),
            dma((seqs, chips - 1)),
            dma((tensors - 1,)),
            dma((tensors - 1,)),
            dma((seqs, tensors - 1)),
            dma((seqs, tensors - 1)),
        ],
        compiler_params=pltpu.CompilerParams(
            collective_id=0, has_side_effects=True, vmem_limit_bytes=60 * 1024 * 1024
        ),
    )
    return call(
        dec_queries, enc_keys, enc_values, out_grad, key_weight, value_weight,
        enc_hidden, enc_gain.reshape(1, feats),
    )


def solution(mesh):
    wide = P("section", "dp", None, "tensor")
    return jax.shard_map(
        functools.partial(per_device, mesh.shape["section"], mesh.shape["tensor"]),
        mesh=mesh,
        in_specs=(
            wide, wide, wide, wide,
            P("section", None, "tensor"),
            P("section", None, "tensor"),
            P("dp", "section", "tensor"),
            P("tensor"),
        ),
        out_specs=P("dp", "section", "tensor"),
        check_vma=False,
    )
```

time: 160 us -> 57.9 us (0.36)
  waiting for transfers between devices: 68.1 us -> 0 us
  Pallas kernels: 0 us -> 56.1 us
  matrix products: 32.5 us -> 0 us
  local copies, waits for them, and re-layouts: 19.4 us -> 1.67 us
  blocking collectives: 16.2 us -> 0 us
  between operations: 13.5 us -> 0.01 us
  other arithmetic: 9.88 us -> 0 us
    reduce_scatter x2 -> x0, waiting for transfers between devices: 68.1 us -> none  [the longest x1 52.8 us: per_device(): lax.psum_scatter(partial_value, 'tensor', scatter_dimension=2, tiled=True)]
    pallas_call x0 -> x1, Pallas kernels: none -> 56.1 us  [per_device(): call(dec_queries, enc_keys, enc_values, out_grad, key_weight, value_weigh...]
    dot_general x5 -> x0, matrix products: 21.9 us -> none  [the longest x1 11.6 us: per_device(): jnp.einsum('bhqk,bqhd->bkhd', score_low, query_heads, preferred_element_t...]
    psum x1 -> x0, blocking collectives: 16.2 us -> none  [per_device(): cross_total = lax.psum(cross_local, 'tensor')]
    sub x1 -> x0, matrix products: 10.7 us -> none  [per_device(): shifted = jnp.exp(scores - jnp.max(scores, axis=-1, keepdims=True))]
    unnamed x19 -> x1, local copies, waits for them, and re-layouts: 9.66 us -> 1.67 us
    convert_element_type x1 -> x0, other arithmetic: 6.84 us -> none  [per_device(): probs_low = attn_probs.astype(jnp.bfloat16)]
    convert_element_type x2 -> x0, local copies, waits for them, and re-layouts: 5.77 us -> none  [the longest x1 3.09 us: per_device(): key_grad = jnp.einsum('bhqk,bqhd->bkhd', score_low, query_heads, preferre...]
  transfers between devices with their start and end apart: 2 -> 0, of which waited for: 2 -> 0; matrix products, arithmetic and copies ran while one was open for 0% -> 0% of each run, Pallas kernels for 0% -> 0%
where the time goes in v1:
time: 57.9 us; the launch traced here: 57.8 us
  Pallas kernels  56.1 us (97%)
  local copies, waits for them, and re-layouts  1.67 us (3%)
    pallas_call x1, Pallas kernels, per_device(): call(dec_queries, enc_keys, enc_values, out_grad, key_weight, value_weigh...  56.1 us
    unnamed x1, local copies, waits for them, and re-layouts  1.67 us

profile of v1, /device:TPU:0, one launch (start us, length us, event | category | flops | bytes accessed | tf_op | source)
XLA Modules:
  0.0 57.8 jit_solution(17586706662473367624)
XLA Ops:
  0.0 56.1 %shard_map.82 = f32[2,256,128]{2,1,0:T(8,128)} custom-call(bf16[1,2,512,1024]{3,2,1,0:T(8,128)(2,1)} %q_hbm.1, bf16[1,2,512,1024]{3,2,1,0:T(8,128)(2,1)} %k_hbm.1, bf16[1,2,512,1024]{3,2,1,0:T(8,128)(2,1)} %v_hbm.1, bf16[1,2,512,1024]{3,2,1,0:T(8,128)(2,1)} %g_hbm.1, bf16[1,1024,1024]{2,1,0:T(8,128)(2,1)} %wk_hbm.1, bf16[1,1024,1024]{2,1,0:T(8,128)(2,1)} %wv_hbm.1, ...), custom_call_target="tpu_custom_call" | custom-call | tf_op jit(solution)/shard_map/pallas_call | solution.py:349
  56.1 1.7 %copy.10 = f32[2,256,128]{2,1,0:T(8,128)} copy(f32[2,256,128]{2,1,0:T(8,128)} %shard_map.82) | data formatting | bytes 524288
